TPU v7x, 8 devices: a whole 2x2x1 slice. The times are simulated.
8 devices in a mesh: dp: 1 (over z), sp: 8 (over x, y, core).
Axes of the slice: x: 2, y: 2, z: 1, core: 2. Of those that a mesh axis runs over, the one named last changes fastest.
Arguments:
- q: bfloat16 [32, 8, 256], P('dp')
- k: bfloat16 [32, 4096, 8, 256], P('dp', 'sp')
- v: bfloat16 [32, 4096, 8, 256], P('dp', 'sp')
Outputs:
- q: bfloat16 [32, 8, 256], P('dp')
All inputs are finite; a program needn't handle non-finite values.
Results may differ from a plain program's by a relative error of at most 0.012.
Values are sent between devices in bfloat16 or wider.
A program may use at most 2 GiB of HBM per device.

v0:
```python
import functools
import math

import jax
import jax.numpy as jnp
from jax import lax
from jax.experimental import pallas as pl
from jax.experimental.pallas import tpu as pltpu
from jax.sharding import PartitionSpec as P

K_SLOTS, V_SLOTS = 7, 7
FLIGHT = 8
LEAD = 4
LATE = 1
PIECES = (8, 4, 4)
TILE = 256
LANES = 128


def peers_of(me):
    x, y, core = me // 4, (me // 2) % 2, me % 2
    for dx, dy, dc in ((1, 1, 0), (1, 1, 1), (1, 0, 0), (1, 0, 1), (0, 1, 0), (0, 1, 1), (0, 0, 1)):
        px = 1 - x if dx else x
        py = 1 - y if dy else y
        pc = 1 - core if dc else core
        yield px * 4 + py * 2 + pc


def kernel(n, q_hbm, k_hbm, v_hbm, o_ref, q_buf, k_buf, v_buf, s_buf, p_buf, sums, parts, stats, q_sem, k_sem, v_sem, piece_sem, send_sem, recv_sem):
    seqs, rows, head = k_hbm.shape
    heads = q_hbm.shape[1]
    tiles = rows // TILE
    log2e_scaled = math.log2(math.e) * head**-0.5
    me = lax.axis_index("sp")
    peers = list(peers_of(me))

    def k_copy(b):
        slot = lax.rem(b, K_SLOTS)
        return pltpu.make_async_copy(k_hbm.at[b], k_buf.at[slot], k_sem.at[slot])

    def v_copy(b):
        slot = lax.rem(b, V_SLOTS)
        return pltpu.make_async_copy(v_hbm.at[b], v_buf.at[slot], v_sem.at[slot])

    def piece_copy(i):
        part = pl.ds(sum(PIECES[:i]) * TILE, PIECES[i] * TILE)
        return pltpu.make_async_copy(v_hbm.at[seqs - 1, part], v_buf.at[(seqs - 1) % V_SLOTS, part], piece_sem.at[i])

    queue = [(k_copy, b) for b in range(LEAD + 1)]
    for b in range(seqs - LEAD - 1):
        queue += [(v_copy, b), (k_copy, b + LEAD + 1)]
    queue += [(v_copy, b) for b in range(seqs - LEAD - 1, seqs - 1)] + [(piece_copy, i) for i in range(len(PIECES))]
    last = len(queue) - len(PIECES)

    def start(first):
        for copy, b in queue[first : first + 1] if first < last else queue[last:] if first == last else ():
            copy(b).start()

    def to(peer, ref, send, recv):
        return pltpu.make_async_remote_copy(
            src_ref=ref, dst_ref=ref, send_sem=send, recv_sem=recv, device_id={"sp": peer}, device_id_type=pl.DeviceIdType.MESH
        )

    start(0)
    pltpu.make_async_copy(q_hbm, q_buf, q_sem).start()
    for i in range(1, FLIGHT):
        start(i)

    barrier = pltpu.get_barrier_semaphore()
    for peer in peers:
        pl.semaphore_signal(barrier, inc=1, device_id={"sp": peer}, device_id_type=pl.DeviceIdType.MESH)

    own = lax.broadcasted_iota(jnp.int32, (heads, TILE), 1) % heads == lax.broadcasted_iota(jnp.int32, (heads, TILE), 0)
    lane = lax.broadcasted_iota(jnp.int32, (heads, LANES), 1)

    def score(b):
        slot = lax.rem(b, K_SLOTS)
        q = q_buf[b]
        for t in range(tiles):
            s = lax.dot_general(q, k_buf[slot, t * TILE : (t + 1) * TILE, :], (((1,), (1,)), ((), ())), preferred_element_type=jnp.float32)
            s_buf[:, t * TILE : (t + 1) * TILE] = jnp.where(own, s, -jnp.inf)

    def weigh(b, stat):
        p_slot = lax.rem(b, LEAD - 1)
        scores = [s_buf[:, t * TILE : (t + 1) * TILE] for t in range(tiles)]
        high = jnp.max(functools.reduce(jnp.maximum, scores), -1, keepdims=True)
        total = None
        for t in range(tiles):
            w = jnp.exp2((scores[t] - high) * log2e_scaled)
            p_buf[p_slot, :, t * TILE : (t + 1) * TILE] = w.astype(jnp.bfloat16)
            total = w if total is None else total + w
        total = jnp.sum(total, -1, keepdims=True)
        return jnp.where(lane == b, high, jnp.where(lane == b + LANES // 2, total, stat))

    def gather_values(b, first, count, total=None):
        slot, p_slot = lax.rem(b, V_SLOTS), lax.rem(b, LEAD - 1)
        for t in range(first, first + count):
            d = jnp.dot(p_buf[p_slot, :, t * TILE : (t + 1) * TILE], v_buf[slot, t * TILE : (t + 1) * TILE, :], preferred_element_type=jnp.float32)
            total = d if total is None else total + d
        return total

    def keep(b, total):
        parts[me, b] = total.astype(jnp.bfloat16)

    def keep_halves(b, pieces, before=lambda i: None):
        halves, begin = [None, None], 0
        for i, count in enumerate(pieces):
            before(i)
            for h in range(2):
                halves[h] = gather_values(b, begin + h * (count // 2), count // 2, halves[h])
            begin += count
        for h in range(2):
            sums[h] = halves[h]
        first = me // n
        keep(b, sums[first] + sums[first + 1])

    pltpu.make_async_copy(q_hbm, q_buf, q_sem).wait()
    stat = jnp.zeros((heads, LANES), jnp.float32)
    for b in range(LEAD):
        k_copy(b).wait()
        start(FLIGHT + b)
        if b >= 1:
            stat = weigh(b - 1, stat)
        score(b)

    def step(b, stat):
        k_copy(b + LEAD).wait()
        if isinstance(b, int):
            start(LEAD + 2 * b + FLIGHT)
        elif FLIGHT % 2:
            v_copy(b + FLIGHT // 2).start()
        else:
            k_copy(b + LEAD + FLIGHT // 2).start()
        v_copy(b).wait()
        if isinstance(b, int):
            start(LEAD + 2 * b + FLIGHT + 1)
        elif FLIGHT % 2:
            k_copy(b + LEAD + FLIGHT // 2 + 1).start()
        else:
            v_copy(b + FLIGHT // 2).start()
        keep(b, gather_values(b, 0, tiles))
        stat = weigh(b + LEAD - 1, stat)
        score(b + LEAD)
        return stat

    def place(b):
        return max(0, b - seqs + LATE + 1)

    def send(first, count, k):
        for peer in peers:
            to(peer, parts.at[me, pl.ds(first, count)], send_sem.at[0], recv_sem.at[k]).start()

    quiet, end = seqs // 4, (last - FLIGHT + 1) // 2 - LEAD
    stat = lax.fori_loop(0, quiet, step, stat)
    pl.semaphore_wait(barrier, n - 1)
    send(0, quiet, 0)

    def step_and_send(b, stat):
        stat = step(b, stat)
        send(b, 1, place(b) if isinstance(b, int) else 0)
        return stat

    stat = lax.fori_loop(quiet, end, step_and_send, stat)
    for b in range(end, seqs - LEAD):
        stat = step_and_send(b, stat)
    for b in range(seqs - LEAD, seqs - 1):
        v_copy(b).wait()
        keep_halves(b, (tiles,))
        if b == seqs - LEAD:
            stats[me] = weigh(seqs - 1, stat)
        send(b, 1, place(b))
        if b == seqs - LEAD:
            for peer in peers:
                to(peer, stats.at[me], send_sem.at[1], recv_sem.at[LATE + 1]).start()
    keep_halves(seqs - 1, PIECES, lambda i: piece_copy(i).wait())
    send(seqs - 1, 1, place(seqs - 1))

    to(peers[0], stats.at[0 : n - 1], send_sem.at[1], recv_sem.at[LATE + 1]).wait()
    seen = [stats[i] for i in range(n)]
    high = functools.reduce(jnp.maximum, seen)
    scale = [jnp.exp2((s - high) * log2e_scaled) for s in seen]
    total = sum(c * pltpu.roll(s, LANES // 2, 1) for c, s in zip(scale, seen))
    scale = [c / total for c in scale]

    def weights_of(b):
        return [jnp.broadcast_to(c[:, b : b + 1], (heads, head)) for c in scale]

    def put(b, weights):
        o_ref[b] = sum(w * parts[i, b].astype(jnp.float32) for i, w in enumerate(weights)).astype(o_ref.dtype)

    late = {b: weights_of(b) for b in range(seqs - LATE, seqs)}
    to(peers[0], parts.at[0 : n - 1, 0 : seqs - LATE], send_sem.at[0], recv_sem.at[0]).wait_recv()
    for b in range(seqs - LATE):
        put(b, weights_of(b))
    for b, weights in late.items():
        to(peers[0], parts.at[0 : n - 1, b], send_sem.at[0], recv_sem.at[place(b)]).wait_recv()
        put(b, weights)
    to(peers[0], parts.at[0 : n - 1], send_sem.at[0], recv_sem.at[0]).wait_send()


def solution(mesh):
    n = mesh.shape["sp"]

    def step(q, k, v):
        seqs, tokens, heads, head = k.shape
        rows = tokens * heads
        return pl.pallas_call(
            functools.partial(kernel, n),
            out_shape=pltpu.VMEM(q.shape, q.dtype),
            in_specs=[pl.BlockSpec(memory_space=pl.ANY)] * 3,
            out_specs=pl.BlockSpec(memory_space=pltpu.VMEM),
            scratch_shapes=[
                pltpu.VMEM(q.shape, q.dtype),
                pltpu.VMEM((K_SLOTS, rows, head), k.dtype),
                pltpu.VMEM((V_SLOTS, rows, head), v.dtype),
                pltpu.VMEM((heads, rows), jnp.float32),
                pltpu.VMEM((LEAD - 1, heads, rows), jnp.bfloat16),
                pltpu.VMEM((2, heads, head), jnp.float32),
                pltpu.VMEM((n, seqs, heads, head), jnp.bfloat16),
                pltpu.VMEM((n, heads, LANES), jnp.float32),
                pltpu.SemaphoreType.DMA,
                pltpu.SemaphoreType.DMA((K_SLOTS,)),
                pltpu.SemaphoreType.DMA((V_SLOTS,)),
                pltpu.SemaphoreType.DMA((len(PIECES),)),
                pltpu.SemaphoreType.DMA((2,)),
                pltpu.SemaphoreType.DMA((LATE + 2,)),
            ],
            compiler_params=pltpu.CompilerParams(collective_id=0, has_side_effects=True),
        )(q, k.reshape(seqs, rows, head), v.reshape(seqs, rows, head))

    return jax.shard_map(
        step,
        mesh=mesh,
        in_specs=(P("dp", None, None), P("dp", "sp", None, None), P("dp", "sp", None, None)),
        out_specs=P("dp", None, None),
        check_vma=False,
    )
```

profile of v0, /device:TPU:0, one launch (start us, length us, event | category | flops | bytes accessed | tf_op | source)
XLA Modules:
  0.0 46.7 jit_solution(4264349376225726478)
XLA Ops:
  0.0 46.0 %shard_map.37 = bf16[32,8,256]{2,1,0:T(8,128)(2,1)S(1)} custom-call(bf16[32,8,256]{2,1,0:T(8,128)(2,1)} %q_hbm.1, bf16[32,4096,256]{2,1,0:T(8,128)(2,1)} %bitcast.k_hbm, bf16[32,4096,256]{2,1,0:T(8,128)(2,1)} %bitcast.1.v_hbm), custom_call_target="tpu_custom_call" | custom-call | tf_op jit(solution)/shard_map/pallas_call | solution.py:207
  46.0 0.7 %copy.5 = bf16[32,8,256]{2,1,0:T(8,128)(2,1)} copy(bf16[32,8,256]{2,1,0:T(8,128)(2,1)S(1)} %shard_map.37) | data formatting | bytes 262144
where the time goes:
time: 46.8 us; the launch traced here: 46.7 us
  Pallas kernels  46 us (98%)
  local copies, waits for them, and re-layouts  0.66 us (1%)
    pallas_call x1, Pallas kernels, step(): pl.pallas_call(functools.partial(kernel, n), out_shape=pltpu.VMEM(q.shape...  46 us

commit v1 on v0

--- a/solution.py
+++ b/solution.py
@@ -8,8 +8,8 @@
 from jax.experimental.pallas import tpu as pltpu
 from jax.sharding import PartitionSpec as P
 
-K_SLOTS, V_SLOTS = 7, 7
-FLIGHT = 8
+K_SLOTS, V_SLOTS = 6, 6
+FLIGHT = 7
 LEAD = 4
 LATE = 1
 PIECES = (8, 4, 4)

time: 46.8 us -> 46.7 us (level)
  no operation moved by 1% of the time
where the time goes in v1:
time: 46.7 us
  Pallas kernels  46 us (99%)
  local copies, waits for them, and re-layouts  0.66 us (1%)
    pallas_call x1, Pallas kernels, step(): pl.pallas_call(functools.partial(kernel, n), out_shape=pltpu.VMEM(q.shape...  46 us

profile of v1, /device:TPU:0, one launch (start us, length us, event | category | flops | bytes accessed | tf_op | source)
XLA Modules:
  0.0 46.7 jit_solution(9610122595343335502)
XLA Ops:
  0.0 46.0 %shard_map.37 = bf16[32,8,256]{2,1,0:T(8,128)(2,1)S(1)} custom-call(bf16[32,8,256]{2,1,0:T(8,128)(2,1)} %q_hbm.1, bf16[32,4096,256]{2,1,0:T(8,128)(2,1)} %bitcast.k_hbm, bf16[32,4096,256]{2,1,0:T(8,128)(2,1)} %bitcast.1.v_hbm), custom_call_target="tpu_custom_call" | custom-call | tf_op jit(solution)/shard_map/pallas_call | solution.py:207
  46.0 0.7 %copy.5 = bf16[32,8,256]{2,1,0:T(8,128)(2,1)} copy(bf16[32,8,256]{2,1,0:T(8,128)(2,1)S(1)} %shard_map.37) | data formatting | bytes 262144
